TPU v7x, 32 devices: a whole 2x2x4 slice. The times are simulated.
32 devices in a mesh: row: 8 (over y, x, core), col: 4 (over z).
Axes of the slice: x: 2, y: 2, z: 4, core: 2. Of those that a mesh axis runs over, the one named last changes fastest.
Arguments:
- homolog_representation: bfloat16 [64, 128, 64], P('row', 'col'), may hold values from -1.5 to 1.5
- pair_state: bfloat16 [128, 128, 128], P('row', 'col'), may hold values from -6 to 6
- homolog_present: int32 [64], replicated, may hold values 0 or 1
- token_live_mask: int32 [128], replicated, may hold values 0 or 1
- product_projection: bfloat16 [64, 64], replicated, may hold values from -0.75 to 0.75
- mean_matrix: bfloat16 [1024, 128], replicated, may hold values from -0.75 to 0.75
- score_matrix: float32 [128, 8], replicated, may hold values from -17.5 to 17.5
- payload_projection: bfloat16 [64, 256], replicated, may hold values from -0.75 to 0.75
- switch_projection: bfloat16 [64, 256], replicated, may hold values from -0.75 to 0.75
- return_projection: bfloat16 [256, 64], replicated, may hold values from -1.5 to 1.5
- transition_input: bfloat16 [128, 1024], replicated, may hold values from -0.5 to 0.5
- transition_output: bfloat16 [512, 128], replicated, may hold values from -0.25 to 0.25
Outputs:
- alignment_output: bfloat16 [64, 128, 64], P('row', 'col')
- pair_output: bfloat16 [128, 128, 128], P('row', 'col')
All inputs are finite; a program needn't handle non-finite values.
Results may differ from a plain program's by a relative error of at most 0.038.
Values may be sent and summed in bfloat16 or wider, within the bound.
No kernel may reach another device: no remote copies, remote signals or barrier semaphores. Data moves between devices by JAX's collectives and lax.ppermute only.
A program may use at most 64 MiB of HBM per device.

v0:
```python
import functools

import jax
import jax.numpy as jnp
from jax import lax
from jax.experimental import pallas as pl
from jax.experimental.pallas import tpu as pltpu
from jax.sharding import PartitionSpec as P

EPS = 1e-05
F32 = jnp.float32
BF16 = jnp.bfloat16
VMEM_LIMIT = 40 * 1024 * 1024


def normed(v):
    center = v - jnp.mean(v, axis=-1, keepdims=True)
    spread = jnp.mean(center * center, axis=-1, keepdims=True)
    return center * lax.rsqrt(spread + EPS)


def lane_iota(shape):
    return lax.broadcasted_iota(jnp.int32, shape, len(shape) - 1)


def mm(a, b, dims=((1,), (0,)), precision=None):
    return lax.dot_general(a, b, (dims, ((), ())), precision=precision, preferred_element_type=F32)


def meet(a, b, cols):
    return a ^ b ^ (cols - 1)


def one_hot_swap(major, minor, transpose=False):
    size = major * minor
    row = lax.broadcasted_iota(jnp.int32, (size, size), 0)
    col = lax.broadcasted_iota(jnp.int32, (size, size), 1)
    if transpose:
        major, minor = minor, major
    return jnp.where((row % minor) * major + row // minor == col, 1.0, 0.0).astype(BF16)


def own_kernel(
    x_ref, wp_ref, present_ref, live_ref,
    xn_ref, proj_ref, w_ref, turn_ref, token_ref, seq_ref, inv_ref, *, width,
):
    row = lax.axis_index("row")
    seqs, col_tok, feat = x_ref.shape
    per = 128 // width
    wp = wp_ref[...]
    w = jnp.concatenate([wp[:, :width]] * per + [wp[:, width:]] * per, axis=1)
    w_ref[...] = w
    turn = one_hot_swap(col_tok, seqs)
    turn_ref[...] = turn
    xn = normed(x_ref[...].astype(F32).reshape(seqs * col_tok, feat)).astype(BF16)
    xn_ref[...] = xn.reshape(xn_ref.shape)
    proj_ref[...] = mm(mm(turn, xn).astype(BF16), w)
    flags = present_ref[...].astype(F32)
    shape = (seqs, flags.shape[1])
    mine = lane_iota(shape) == row * seqs + lax.broadcasted_iota(jnp.int32, shape, 0)
    own_flags = jnp.sum(jnp.where(mine, flags, 0.0), axis=1, keepdims=True)
    seq_ref[...] = jnp.broadcast_to(own_flags, seq_ref.shape)
    live = live_ref[...].astype(F32)
    tokens = live.shape[1]
    shape = (token_ref.shape[0], tokens)
    here = lane_iota(shape) // per == lax.broadcasted_iota(jnp.int32, shape, 0)
    shape = (tokens, 128)
    spread = lax.broadcasted_iota(jnp.int32, shape, 0) % per == lane_iota(shape) // width
    token_ref[...] = mm(
        jnp.where(here, live, 0.0).astype(BF16), jnp.where(spread, 1.0, 0.0).astype(BF16)
    )
    count = jnp.sum(flags, axis=1, keepdims=True)
    inv_ref[...] = jnp.broadcast_to(1.0 / jnp.maximum(count, 1.0), inv_ref.shape)


def pack_kernel(*refs, cols, rows, col_tok, row_tok, width):
    xs = refs[: cols - 1]
    own_ref, proj_ref, w_ref, turn_ref, token_ref, seq_ref, send_ref, xn_ref = refs[cols - 1 :]
    col = lax.axis_index("col")
    seqs = own_ref.shape[0]
    block = seqs * col_tok
    per = 128 // width
    per_col = col_tok // row_tok
    left_tiles = row_tok // per
    right_tiles = col_tok // per
    other = (left_tiles + right_tiles) * 128
    gran = lane_iota((seqs, 128)) // width
    present = seq_ref[...]

    def tile(y, t):
        out = None
        for g in range(per):
            part = y[(t * per + g) * seqs : (t * per + g + 1) * seqs, :]
            out = part if out is None else jnp.where(gran == g, part, out)
        return out

    for k in range(cols):
        at = lax.rem(col - k + cols, cols)
        if k == 0:
            xn_ref[at] = own_ref[...]
            y = proj_ref[...]
        else:
            v = xs[k - 1][...]
            xn = normed(v.astype(F32).reshape(block, v.shape[2])).astype(BF16)
            xn_ref[at] = xn.reshape(xn_ref.shape[1:])
            y = mm(mm(turn_ref[...], xn).astype(BF16), w_ref[...])
        left = y[:, :128]
        right = y[:, 128:]
        for t in range(right_tiles):
            mask = token_ref[pl.ds(at * right_tiles + t, 1), :]
            lanes = (left_tiles + t) * 128
            v = (tile(right, t) * mask).astype(BF16)
            for e in range(per_col):
                send_ref[meet(at, col, cols) * per_col + e, :, lanes : lanes + 128] = v
            if k == 0:
                for r in range(rows):
                    send_ref[r, :, other + lanes : other + lanes + 128] = v
            sub = t // left_tiles
            lanes = (t % left_tiles) * 128
            v = (tile(left, t) * (mask * present)).astype(BF16)
            send_ref[at * per_col + sub, :, other + lanes : other + lanes + 128] = v
            if k == 0:
                for r in range(sub, rows, per_col):
                    send_ref[r, :, lanes : lanes + 128] = v


def values_kernel(xn_ref, own_ref, wv_ref, wg_ref, values_ref, gate_ref):
    cols, seqs, col_tok, feat = xn_ref.shape
    mixed = wv_ref.shape[1]
    for k in range(cols):
        v = mm(xn_ref[k].reshape(seqs * col_tok, feat), wv_ref[...]).reshape(seqs, col_tok, mixed)
        values_ref[:, k * col_tok : (k + 1) * col_tok, :] = v.astype(BF16)
    gate = mm(own_ref[...].reshape(seqs * col_tok, feat), wg_ref[...])
    gate_ref[...] = 1.0 / (1.0 + jnp.exp(-gate))


def order_kernel(pair_ref, other_ref, swap_ref, own_out, other_out):
    row_tok, col_tok, width = pair_ref.shape
    swap_ref[...] = one_hot_swap(row_tok, col_tok)
    back = one_hot_swap(row_tok, col_tok, transpose=True)
    for source, target in ((pair_ref, own_out), (other_ref, other_out)):
        target[...] = mm(back, source[...].reshape(row_tok * col_tok, width)).astype(BF16)


def pair_mid(got, state, mean_ref, swap, inv, row_tok, col_tok, width):
    per = 128 // width
    left = mm(got[:, : row_tok * width], swap).astype(BF16)
    right = got[:, row_tok * width :]
    gran = lane_iota((row_tok, 128)) // width
    group = per * row_tok
    delta = None
    for pair in range(0, width // per, 2):
        outer = mm(left[:, pair * group : (pair + 2) * group], right, ((0,), (0,)))
        outer = (outer * inv).astype(BF16)
        halves = []
        for half in range(2):
            tiles = []
            for jh in range(col_tok // per):
                a = []
                for lo in range(per):
                    at = (half * per + lo) * row_tok
                    a.append(outer[at : at + row_tok, jh * 128 : (jh + 1) * 128])
                step = 1
                while step < per:
                    odd = (gran // step) % 2 == 1
                    b = list(a)
                    for lo in range(per):
                        if (lo // step) % 2 == 0:
                            b[lo] = jnp.where(odd, pltpu.roll(a[lo + step], step * width, 1), a[lo])
                            b[lo + step] = jnp.where(odd, a[lo + step], pltpu.roll(a[lo], 128 - step * width, 1))
                    a = b
                    step *= 2
                tiles += a
            halves.append(jnp.concatenate(tiles, axis=0))
        part = mm(jnp.concatenate(halves, axis=1), mean_ref[pair * 128 : (pair + 2) * 128, :])
        delta = part if delta is None else delta + part
    return (state.astype(F32) + delta).astype(BF16)


def score_kernel(
    got_ref, state_ref, mean_ref, swap_ref, score_ref, inv_ref, chunk_ref, *, row_tok, col_tok, width, heads
):
    rows, seqs, lanes = got_ref.shape
    got = got_ref[:, :, : lanes // 2].reshape(rows * seqs, lanes // 2)
    mid = pair_mid(got, state_ref[...], mean_ref, swap_ref[...], inv_ref[:1, :1], row_tok, col_tok, width)
    pn = normed(mid.astype(F32))
    scores = mm(score_ref[...], pn, ((1,), (1,)), lax.Precision.HIGHEST)
    sub = lax.broadcasted_iota(jnp.int32, (heads, 128), 0)
    lane_gran = lane_iota((heads, 128)) // row_tok
    turn = jnp.bitwise_and(lane_gran - sub, heads - 1)
    tiles = []
    for t in range(col_tok // heads):
        v = scores[:, t * 128 : (t + 1) * 128]
        out = v
        for k in range(1, heads):
            moved = pltpu.roll(pltpu.roll(v, heads - k, 0), row_tok * k, 1)
            out = jnp.where(turn == k, moved, out)
        tiles.append(out)
    by_token = jnp.concatenate(tiles, axis=0)
    top = jnp.max(by_token, axis=0, keepdims=True).astype(BF16)
    shifted = jnp.exp(by_token - top.astype(F32)).astype(BF16)
    tops = jnp.broadcast_to(top, (8, 128))
    for d in range(chunk_ref.shape[0]):
        chunk_ref[d, :col_tok, :] = shifted
        chunk_ref[d, col_tok:, :] = tops


def transition_kernel(
    got_ref, state_ref, mean_ref, swap_ref, inv_ref, win_ref, wout_ref, out_ref, *, row_tok, col_tok, width
):
    rows, seqs, lanes = got_ref.shape
    got = got_ref[:, :, lanes // 2 :].reshape(rows * seqs, lanes // 2)
    swap = swap_ref[...]
    mid = pair_mid(got, state_ref[...], mean_ref, swap, inv_ref[:1, :1], row_tok, col_tok, width).astype(F32)
    pn = normed(mid).astype(BF16)
    ff = wout_ref.shape[0]
    step = 8 * row_tok
    news = []
    for b in range(col_tok // 8):
        pre = mm(pn[b * step : (b + 1) * step, :], win_ref[...])
        act = pre[:, :ff]
        hidden = (act / (1.0 + jnp.exp(-act)) * pre[:, ff:]).astype(BF16)
        news.append((mid[b * step : (b + 1) * step, :] + mm(hidden, wout_ref[...])).astype(BF16))
    out_ref[...] = mm(swap, jnp.concatenate(news, axis=0)).astype(BF16).reshape(out_ref.shape)


def blend_kernel(
    got_ref, values_ref, gate_ref, x_ref, wr_ref, live_ref, pair_ref, out_ref, pair_out, pair_sem,
    *, cols, per_col, row_tok, col_tok, heads,
):
    leave = pltpu.make_async_copy(pair_ref, pair_out, pair_sem)
    leave.start()
    own = lax.axis_index("col")
    lanes = []
    for q in range(per_col):
        froms = [meet(k, own, cols) * per_col + q for k in range(cols)]
        tops = [got_ref[f, col_tok:, :].astype(F32)[:1] for f in froms]
        top = functools.reduce(jnp.maximum, tops)
        parts = [got_ref[f, :col_tok, :].astype(F32) * jnp.exp(t - top) for f, t in zip(froms, tops)]
        whole = functools.reduce(lambda a, b: a + b, [jnp.sum(p, axis=0, keepdims=True) for p in parts])
        lanes.append(jnp.concatenate(parts, axis=0) / whole)
    weights = jnp.concatenate([jnp.transpose(v) for v in lanes], axis=0)
    weights = (weights * live_ref[...].astype(F32)).astype(BF16)
    mixed = values_ref.shape[2]
    head_of = lane_iota((row_tok, mixed)) // (mixed // heads)
    seqs = values_ref.shape[0]
    blocks = []
    for s in range(seqs):
        full = mm(weights, values_ref[s])
        for q in range(per_col):
            acc = None
            for h in range(heads):
                at = (q * heads + h) * row_tok
                part = full[at : at + row_tok, :]
                acc = part if acc is None else jnp.where(head_of == h, part, acc)
            blocks.append(acc)
    average = jnp.concatenate(blocks, axis=0)
    gated = (gate_ref[...] * average).astype(BF16)
    delta = mm(gated, wr_ref[...], ((1,), (1,))).reshape(x_ref.shape)
    out_ref[...] = (x_ref[...].astype(F32) + delta).astype(BF16)
    leave.wait()


def call(kernel, outs, ins, scratch=(), hbm_outs=0, flops=0, **keys):
    return pl.pallas_call(
        functools.partial(kernel, **keys),
        out_shape=tuple(jax.ShapeDtypeStruct(shape, dtype) for shape, dtype in outs),
        in_specs=[pl.BlockSpec(memory_space=pltpu.VMEM)] * len(ins),
        out_specs=(pl.BlockSpec(memory_space=pltpu.VMEM),) * (len(outs) - hbm_outs)
        + (pl.BlockSpec(memory_space=pl.ANY),) * hbm_outs,
        scratch_shapes=list(scratch),
        compiler_params=pltpu.CompilerParams(vmem_limit_bytes=VMEM_LIMIT),
        cost_estimate=pl.CostEstimate(flops=flops, bytes_accessed=0, transcendentals=0) if flops else None,
    )(*ins)


def body(x, pair, present, live, wp, mean, score, wv, wg, wr, win, wout):
    cols = lax.axis_size("col")
    rows = lax.axis_size("row")
    seqs, col_tok, feat = x.shape
    row_tok, _, pair_width = pair.shape
    width = wp.shape[1] // 2
    heads = score.shape[1]
    mixed = wv.shape[1]
    tokens = cols * col_tok
    per_col = col_tok // row_tok
    assert col_tok % row_tok == 0 and rows == per_col * cols and cols & (cols - 1) == 0
    assert heads * row_tok == 128 and 128 % width == 0 and width == col_tok
    mine = seqs * col_tok
    lanes = 2 * (row_tok + col_tok) * width

    swap = [
        (r * cols + c, (meet(r // per_col, c, cols) * per_col + r % per_col) * cols + r // per_col)
        for r in range(rows)
        for c in range(cols)
    ]
    xs = [lax.ppermute(x, "col", [(i, (i + k) % cols) for i in range(cols)]) for k in range(1, cols)]
    other_pair = lax.ppermute(pair, ("row", "col"), swap)

    own, proj, w, turn, token, seq, inv = call(
        own_kernel,
        [
            (x.shape, BF16), ((mine, 256), F32), ((feat, 256), BF16), ((mine, mine), BF16),
            ((tokens * width // 128, 128), F32), ((seqs, 128), F32), ((8, 128), F32),
        ],
        [x, wp, present.reshape(1, -1), live.reshape(1, -1)],
        flops=30_000_000, width=width,
    )
    send, xn = call(
        pack_kernel,
        [((rows, seqs, lanes), BF16), ((cols, seqs, col_tok, feat), BF16)],
        xs + [own, proj, w, turn, token, seq],
        cols=cols, rows=rows, col_tok=col_tok, row_tok=row_tok, width=width,
    )
    got = lax.all_to_all(send, "row", 0, 0)
    values, gate = call(
        values_kernel, [((seqs, tokens, mixed), BF16), ((mine, mixed), F32)], [xn, own, wv, wg], flops=100_000_000
    )
    pairs = row_tok * col_tok
    swap_matrix, state, other_state = call(
        order_kernel,
        [((pairs, pairs), BF16), ((pairs, pair_width), BF16), ((pairs, pair_width), BF16)],
        [pair, other_pair],
        flops=100_000_000,
    )
    sizes = dict(row_tok=row_tok, col_tok=col_tok, width=width)
    (chunk,) = call(
        score_kernel,
        [((rows, col_tok + 8, 128), BF16)],
        [got, other_state, mean, swap_matrix, score.T, inv],
        heads=heads, **sizes,
    )
    scores = lax.all_to_all(chunk, "row", 0, 0)
    (pair_new,) = call(
        transition_kernel,
        [(pair.shape, BF16)],
        [got, state, mean, swap_matrix, inv, win, wout],
        flops=1_000_000_000, **sizes,
    )
    alignment, pair_output = call(
        blend_kernel,
        [(x.shape, BF16), (pair.shape, BF16)],
        [scores, values, gate, x, wr.T, live.reshape(1, -1), pair_new],
        scratch=[pltpu.SemaphoreType.DMA], hbm_outs=1, cols=cols, per_col=per_col, row_tok=row_tok, col_tok=col_tok, heads=heads,
    )
    return alignment, pair_output


def solution(mesh):
    spread = P("row", "col", None)
    return jax.shard_map(
        body,
        mesh=mesh,
        in_specs=(spread, spread) + (P(),) * 10,
        out_specs=(spread, spread),
        check_vma=False,
    )
```

profile of v0, /device:TPU:0, one launch (start us, length us, event | category | flops | bytes accessed | tf_op | source)
XLA Modules:
  0.0 45.8 jit_solution(191283265281008735)
XLA Ops:
  0.6 5.1 %collective-permute-start.2 = (bf16[8,32,64]{2,1,0:T(8,128)(2,1)}, bf16[8,32,64]{2,1,0:T(8,128)(2,1)S(1)}, u32[]{:S(2)}, u32[]{:S(2)}) collective-permute-start(bf16[8,32,64]{2,1,0:T(8,128)(2,1)} %x_ref.3), channel_id=1, source_target_pairs={{0,3},{1,0},{2,1},{3,2},{4,7},{5,4},{6,5},{7,6},{8,11},{9,8},{10,9... | collective-permute-start | bytes 98312 | tf_op jit(solution)/shard_map/ppermute | solution.py:297
  5.8 0.0 collective-permute-start.1
  5.8 1.0 %collective-permute-start = (bf16[8,32,64]{2,1,0:T(8,128)(2,1)}, bf16[8,32,64]{2,1,0:T(8,128)(2,1)S(1)}, u32[]{:S(2)}, u32[]{:S(2)}) collective-permute-start(bf16[8,32,64]{2,1,0:T(8,128)(2,1)} %x_ref.3), channel_id=1, source_target_pairs={{0,1},{1,2},{2,3},{3,0},{4,5},{5,6},{6,7},{7,4},{8,9},{9,10},{10,1... | collective-permute-start | bytes 98312 | tf_op jit(solution)/shard_map/ppermute | solution.py:297
  6.8 0.7 %copy-done.7 = s32[128]{0:T(128)S(1)} copy-done((s32[128]{0:T(128)S(1)}, s32[128]{0:T(128)}, u32[]{:S(2)}) %copy-start.7) | copy-done | bytes 536
  7.4 0.0 copy-done.12
  7.4 0.8 %copy-done.1 = bf16[8,32,64]{2,1,0:T(8,128)(2,1)S(1)} copy-done((bf16[8,32,64]{2,1,0:T(8,128)(2,1)S(1)}, bf16[8,32,64]{2,1,0:T(8,128)(2,1)}, u32[]{:S(2)}) %copy-start.1) | copy-done | bytes 32792
  8.3 0.7 %copy-done.11 = bf16[64,64]{1,0:T(8,128)(2,1)S(1)} copy-done((bf16[64,64]{1,0:T(8,128)(2,1)S(1)}, bf16[64,64]{1,0:T(8,128)(2,1)}, u32[]{:S(2)}) %copy-start.11) | copy-done | bytes 8216
  9.0 0.5 %shard_map.131 = (bf16[8,32,64]{2,1,0:T(8,128)(2,1)S(1)}, f32[256,256]{1,0:T(8,128)S(1)}, bf16[64,256]{1,0:T(8,128)(2,1)S(1)}, bf16[256,256]{1,0:T(8,128)(2,1)S(...) custom-call(bf16[8,32,64]{2,1,0:T(8,128)(2,1)S(1)} %copy-done.1, ...), custom_call_target="tpu_custom_call" | custom-call | flops 30000000 | tf_op jit(solution)/shard_map/pallas_call | solution.py:265
  9.5 0.0 collective-permute-done.2.refs_2_
  9.5 2.9 %collective-permute-done.1.refs_1_ = bf16[8,32,64]{2,1,0:T(8,128)(2,1)S(1)} collective-permute-done((bf16[8,32,64]{2,1,0:T(8,128)(2,1)}, bf16[8,32,64]{2,1,0:T(8,128)(2,1)S(1)}, u32[]{:S(2)}, u32[]{:S(2)}) %collective-permute-start.1) | collective-permute-done | bytes 32800 | tf_op jit(solution)/shard_map/ppermute | solution.py:297
  12.4 0.0 collective-permute-done.refs_0_
  12.4 1.5 %shard_map.132 = (bf16[8,8,3072]{2,1,0:T(8,128)(2,1)}, bf16[4,8,32,64]{3,2,1,0:T(8,128)(2,1)S(1)}) custom-call(bf16[8,32,64]{2,1,0:T(8,128)(2,1)S(1)} %collective-permute-done.refs_0_, bf16[8,32,64]{2,1,0:T(8,128)(2,1)S(1)} %collective-permute-done.1.refs_1_, bf16[8,32,64]{2,1,0:T(8,128)(2,1)S(1)} %collective-permute-done.2.refs_2_, ...), custom_call_target="tpu_custom_call" | custom-call | tf_op jit(solution)/shard_map/pallas_call | solution.py:265
  14.0 3.9 %all-to-all-start = ((bf16[8,8,3072]{2,1,0:T(8,128)(2,1)}), bf16[8,8,3072]{2,1,0:T(8,128)(2,1)S(1)}, u32[]{:S(2)}, u32[]{:S(2)}) async-start(bf16[8,8,3072]{2,1,0:T(8,128)(2,1)} %get-tuple-element.22), calls=%async_computation | async-start | bytes 786432 | tf_op jit(solution)/shard_map/all_to_all | solution.py:315
  17.8 0.0 copy-done.9
  17.8 4.8 %collective-permute-start.3 = (bf16[16,32,128]{2,1,0:T(8,128)(2,1)S(1)}, bf16[16,32,128]{2,1,0:T(8,128)(2,1)S(1)}, u32[]{:S(2)}, u32[]{:S(2)}) collective-permute-start(bf16[16,32,128]{2,1,0:T(8,128)(2,1)S(1)} %copy-done.9), channel_id=1, source_target_pairs={{0,24},{1,16},{2,8},{3,0},{4,28},{5,20},{6,12},{7,4},{8,17},{9,25}... | collective-permute-start | bytes 393224 | tf_op jit(solution)/shard_map/ppermute | solution.py:298
  22.7 0.0 copy-done.3
  22.7 0.3 shard_map.135
  23.0 0.0 copy-start
  23.0 4.6 %collective-permute-done.3.other_ref = bf16[16,32,128]{2,1,0:T(8,128)(2,1)S(1)} collective-permute-done((bf16[16,32,128]{2,1,0:T(8,128)(2,1)S(1)}, bf16[16,32,128]{2,1,0:T(8,128)(2,1)S(1)}, u32[]{:S(2)}, u32[]{:S(2)}) %collective-permute-start.3) | collective-permute-done | bytes 131104 | tf_op jit(solution)/shard_map/ppermute | solution.py:298
  27.6 0.5 %shard_map.133 = (bf16[512,512]{1,0:T(8,128)(2,1)S(1)}, bf16[512,128]{1,0:T(8,128)(2,1)S(1)}, bf16[512,128]{1,0:T(8,128)(2,1)S(1)}) custom-call(bf16[16,32,128]{2,1,0:T(8,128)(2,1)S(1)} %copy-done.9, bf16[16,32,128]{2,1,0:T(8,128)(2,1)S(1)} %collective-permute-done.3.other_ref), custom_call_target="tpu_custom_call" | custom-call | flops 100000000 | tf_op jit(solution)/shard_map/pallas_call | solution.py:265
  28.1 0.0 copy-start.6
  28.1 0.0 all-to-all-done.got_ref
  28.1 0.0 copy-done
  28.1 0.7 %copy-done.6 = f32[128,8]{0,1:T(8,128)S(1)} copy-done((f32[128,8]{0,1:T(8,128)S(1)}, f32[128,8]{0,1:T(8,128)}, u32[]{:S(2)}) %copy-start.6) | copy-done | bytes 4120
  28.8 3.0 %shard_map.134 = bf16[8,40,128]{2,1,0:T(8,128)(2,1)} custom-call(bf16[8,8,3072]{2,1,0:T(8,128)(2,1)S(1)} %all-to-all-done.got_ref, bf16[512,128]{1,0:T(8,128)(2,1)S(1)} %get-tuple-element.23.state_ref, bf16[1024,128]{1,0:T(8,128)(2,1)S(1)} %copy-done, bf16[512,512]{1,0:T(8,128)(2,1)S(1)} %get-tuple-element.24.swap_ref, f32[8,128]{1,0:T(8,128)S(1)} %bitcast.5, ...), custom_call_target="tpu_custom_call" | custom-call | tf_op jit(solution)/shard_map/pallas_call | solution.py:265
  31.8 7.6 %all-to-all-start.1 = ((bf16[8,40,128]{2,1,0:T(8,128)(2,1)}), bf16[8,40,128]{2,1,0:T(8,128)(2,1)S(1)}, u32[]{:S(2)}, u32[]{:S(2)}) async-start(bf16[8,40,128]{2,1,0:T(8,128)(2,1)} %shard_map.134), calls=%async_computation.1 | async-start | bytes 163840 | tf_op jit(solution)/shard_map/all_to_all | solution.py:333
  39.4 0.0 copy-start.2
  39.4 0.0 copy-start.5
  39.4 3.4 %shard_map.136.pair_ref = bf16[16,32,128]{2,1,0:T(8,128)(2,1)S(1)} custom-call(bf16[8,8,3072]{2,1,0:T(8,128)(2,1)S(1)} %all-to-all-done.got_ref, bf16[512,128]{1,0:T(8,128)(2,1)S(1)} %get-tuple-element.29.state_ref, bf16[1024,128]{1,0:T(8,128)(2,1)S(1)} %copy-done, bf16[512,512]{1,0:T(8,128)(2,1)S(1)} %get-tuple-element.24.swap_ref, ...), custom_call_target="tpu_custom_call" | custom-call | flops 1000000000 | tf_op jit(solution)/shard_map/pallas_call | solution.py:265
  42.8 1.7 %all-to-all-done.1.got_ref = bf16[8,40,128]{2,1,0:T(8,128)(2,1)S(1)} async-done(((bf16[8,40,128]{2,1,0:T(8,128)(2,1)}), bf16[8,40,128]{2,1,0:T(8,128)(2,1)S(1)}, u32[]{:S(2)}, u32[]{:S(2)}) %all-to-all-start.1) | async-done | bytes 81952 | tf_op jit(solution)/shard_map/all_to_all | solution.py:333
  44.5 0.0 copy-done.5
  44.5 1.3 %shard_map.137 = (bf16[8,32,64]{2,1,0:T(8,128)(2,1)}, bf16[16,32,128]{2,1,0:T(8,128)(2,1)}) custom-call(bf16[8,40,128]{2,1,0:T(8,128)(2,1)S(1)} %all-to-all-done.1.got_ref, bf16[8,128,256]{2,1,0:T(8,128)(2,1)S(1)} %get-tuple-element.27.values_ref, f32[256,256]{1,0:T(8,128)S(1)} %get-tuple-element.28.gate_ref, bf16[8,32,64]{2,1,0:T(8,128)(2,1)S(1)} %copy-done.2, ...), custom_call_target="tpu_custom_call" | custom-call | tf_op jit(solution)/shard_map/pallas_call | solution.py:265
  (13 shorter events, 0.0 us)
Async XLA Ops:
  0.6 8.9 %collective-permute-start.2 = (bf16[8,32,64]{2,1,0:T(8,128)(2,1)}, bf16[8,32,64]{2,1,0:T(8,128)(2,1)S(1)}, u32[]{:S(2)}, u32[]{:S(2)}) collective-permute-start(bf16[8,32,64]{2,1,0:T(8,128)(2,1)} %x_ref.3), channel_id=1, source_target_pairs={{0,3},{1,0},{2,1},{3,2},{4,7},{5,4},{6,5},{7,6},{8,11},{9,8},{10,9... | collective-permute-start | bytes 98312 | tf_op jit(solution)/shard_map/ppermute | solution.py:297
  5.8 6.7 %collective-permute-start.1 = (bf16[8,32,64]{2,1,0:T(8,128)(2,1)}, bf16[8,32,64]{2,1,0:T(8,128)(2,1)S(1)}, u32[]{:S(2)}, u32[]{:S(2)}) collective-permute-start(bf16[8,32,64]{2,1,0:T(8,128)(2,1)} %x_ref.3), channel_id=1, source_target_pairs={{0,2},{1,3},{2,0},{3,1},{4,6},{5,7},{6,4},{7,5},{8,10},{9,11},{10,... | collective-permute-start | bytes 98312 | tf_op jit(solution)/shard_map/ppermute | solution.py:297
  5.8 6.7 %collective-permute-start = (bf16[8,32,64]{2,1,0:T(8,128)(2,1)}, bf16[8,32,64]{2,1,0:T(8,128)(2,1)S(1)}, u32[]{:S(2)}, u32[]{:S(2)}) collective-permute-start(bf16[8,32,64]{2,1,0:T(8,128)(2,1)} %x_ref.3), channel_id=1, source_target_pairs={{0,1},{1,2},{2,3},{3,0},{4,5},{5,6},{6,7},{7,4},{8,9},{9,10},{10,1... | collective-permute-start | bytes 98312 | tf_op jit(solution)/shard_map/ppermute | solution.py:297
  6.8 0.7 %copy-start.7 = (s32[128]{0:T(128)S(1)}, s32[128]{0:T(128)}, u32[]{:S(2)}) copy-start(s32[128]{0:T(128)} %param.15) | copy-start | bytes 1540
  6.8 0.7 %copy-start.12 = (s32[64]{0:T(128)S(1)}, s32[64]{0:T(128)}, u32[]{:S(2)}) copy-start(s32[64]{0:T(128)} %param.14) | copy-start | bytes 772
  7.4 0.8 %copy-start.1 = (bf16[8,32,64]{2,1,0:T(8,128)(2,1)S(1)}, bf16[8,32,64]{2,1,0:T(8,128)(2,1)}, u32[]{:S(2)}) copy-start(bf16[8,32,64]{2,1,0:T(8,128)(2,1)} %x_ref.3) | copy-start | bytes 98308
  8.3 0.7 %copy-start.11 = (bf16[64,64]{1,0:T(8,128)(2,1)S(1)}, bf16[64,64]{1,0:T(8,128)(2,1)}, u32[]{:S(2)}) copy-start(bf16[64,64]{1,0:T(8,128)(2,1)} %wp_ref.1) | copy-start | bytes 24580
  14.0 3.9 %copy-start.9 = (bf16[16,32,128]{2,1,0:T(8,128)(2,1)S(1)}, bf16[16,32,128]{2,1,0:T(8,128)(2,1)}, u32[]{:S(2)}) copy-start(bf16[16,32,128]{2,1,0:T(8,128)(2,1)} %pair_ref.1) | copy-start | bytes 393220
  14.0 8.7 %copy-start.3 = (bf16[64,256]{1,0:T(8,128)(2,1)S(1)}, bf16[64,256]{1,0:T(8,128)(2,1)}, u32[]{:S(2)}) copy-start(bf16[64,256]{1,0:T(8,128)(2,1)} %wv_ref.1) | copy-start | bytes 98308
  14.0 8.7 %copy-start.4 = (bf16[64,256]{1,0:T(8,128)(2,1)S(1)}, bf16[64,256]{1,0:T(8,128)(2,1)}, u32[]{:S(2)}) copy-start(bf16[64,256]{1,0:T(8,128)(2,1)} %wg_ref.1) | copy-start | bytes 98308
  14.0 14.1 %all-to-all-start = ((bf16[8,8,3072]{2,1,0:T(8,128)(2,1)}), bf16[8,8,3072]{2,1,0:T(8,128)(2,1)S(1)}, u32[]{:S(2)}, u32[]{:S(2)}) async-start(bf16[8,8,3072]{2,1,0:T(8,128)(2,1)} %get-tuple-element.22), calls=%async_computation | async-start | bytes 786432 | tf_op jit(solution)/shard_map/all_to_all | solution.py:315
  17.8 9.8 %collective-permute-start.3 = (bf16[16,32,128]{2,1,0:T(8,128)(2,1)S(1)}, bf16[16,32,128]{2,1,0:T(8,128)(2,1)S(1)}, u32[]{:S(2)}, u32[]{:S(2)}) collective-permute-start(bf16[16,32,128]{2,1,0:T(8,128)(2,1)S(1)} %copy-done.9), channel_id=1, source_target_pairs={{0,24},{1,16},{2,8},{3,0},{4,28},{5,20},{6,12},{7,4},{8,17},{9,25}... | collective-permute-start | bytes 393224 | tf_op jit(solution)/shard_map/ppermute | solution.py:298
  23.0 5.1 %copy-start = (bf16[1024,128]{1,0:T(8,128)(2,1)S(1)}, bf16[1024,128]{1,0:T(8,128)(2,1)}, u32[]{:S(2)}) copy-start(bf16[1024,128]{1,0:T(8,128)(2,1)} %mean_ref.3) | copy-start | bytes 786436
  28.1 0.7 %copy-start.6 = (f32[128,8]{0,1:T(8,128)S(1)}, f32[128,8]{0,1:T(8,128)}, u32[]{:S(2)}) copy-start(f32[128,8]{0,1:T(8,128)} %param.18) | copy-start | bytes 12292
  28.8 10.6 %copy-start.8 = (bf16[128,1024]{1,0:T(8,128)(2,1)S(1)}, bf16[128,1024]{1,0:T(8,128)(2,1)}, u32[]{:S(2)}) copy-start(bf16[128,1024]{1,0:T(8,128)(2,1)} %win_ref.1) | copy-start | bytes 786436
  31.8 7.6 %copy-start.10 = (bf16[512,128]{1,0:T(8,128)(2,1)S(1)}, bf16[512,128]{1,0:T(8,128)(2,1)}, u32[]{:S(2)}) copy-start(bf16[512,128]{1,0:T(8,128)(2,1)} %wout_ref.1) | copy-start | bytes 393220
  31.8 12.7 %all-to-all-start.1 = ((bf16[8,40,128]{2,1,0:T(8,128)(2,1)}), bf16[8,40,128]{2,1,0:T(8,128)(2,1)S(1)}, u32[]{:S(2)}, u32[]{:S(2)}) async-start(bf16[8,40,128]{2,1,0:T(8,128)(2,1)} %shard_map.134), calls=%async_computation.1 | async-start | bytes 163840 | tf_op jit(solution)/shard_map/all_to_all | solution.py:333
  39.4 5.1 %copy-start.2 = (bf16[8,32,64]{2,1,0:T(8,128)(2,1)S(1)}, bf16[8,32,64]{2,1,0:T(8,128)(2,1)}, u32[]{:S(2)}) copy-start(bf16[8,32,64]{2,1,0:T(8,128)(2,1)} %x_ref.3) | copy-start | bytes 98308
  39.4 5.1 %copy-start.5 = (bf16[256,64]{0,1:T(8,128)(2,1)S(1)}, bf16[256,64]{0,1:T(8,128)(2,1)}, u32[]{:S(2)}) copy-start(bf16[256,64]{0,1:T(8,128)(2,1)} %param.21) | copy-start | bytes 98308
where the time goes:
time: 46.3 us; the launch traced here: 45.8 us
  starting transfers between devices  22.4 us (48%)
  Pallas kernels  10.5 us (23%)
  waiting for transfers between devices  9.22 us (20%)
  local copies, waits for them, and re-layouts  2.93 us (6%)
  between operations  0.76 us (2%)
    pallas_call x7, Pallas kernels, call(): pl.pallas_call(functools.partial(kernel, **keys), out_shape=tuple((jax.Sh...  10.5 us
    all_to_all x1, starting transfers between devices, body(): scores = lax.all_to_all(chunk, 'row', 0, 0)  7.55 us
    ppermute x3, starting transfers between devices, body(): lax.ppermute(x, 'col', [(i, (i + k) % cols) for i in range(cols)])  6.14 us
    ppermute x1, starting transfers between devices, body(): other_pair = lax.ppermute(pair, ('row', 'col'), swap)  4.82 us
    ppermute x1, waiting for transfers between devices, body(): other_pair = lax.ppermute(pair, ('row', 'col'), swap)  4.6 us
    all_to_all x1, starting transfers between devices, body(): got = lax.all_to_all(send, 'row', 0, 0)  3.85 us
    unnamed x26, local copies, waits for them, and re-layouts  2.93 us
    ppermute x3, waiting for transfers between devices, body(): lax.ppermute(x, 'col', [(i, (i + k) % cols) for i in range(cols)])  2.92 us
  transfers between devices with their start and end apart: 6, of which 3 were waited for; matrix products, arithmetic and copies ran while one was open for 0% of the time, Pallas kernels for 10%

commit v1 on v0

--- a/solution.py
+++ b/solution.py
@@ -40,9 +40,13 @@
     return jnp.where((row % minor) * major + row // minor == col, 1.0, 0.0).astype(BF16)
 
 
+def turn_kernel(turn_ref, *, seqs, col_tok):
+    turn_ref[...] = one_hot_swap(col_tok, seqs)
+
+
 def own_kernel(
-    x_ref, wp_ref, present_ref, live_ref,
-    xn_ref, proj_ref, w_ref, turn_ref, token_ref, seq_ref, inv_ref, *, width,
+    x_ref, wp_ref, present_ref, live_ref, turn_ref,
+    xn_ref, proj_ref, w_ref, token_ref, seq_ref, inv_ref, *, width,
 ):
     row = lax.axis_index("row")
     seqs, col_tok, feat = x_ref.shape
@@ -50,8 +54,7 @@
     wp = wp_ref[...]
     w = jnp.concatenate([wp[:, :width]] * per + [wp[:, width:]] * per, axis=1)
     w_ref[...] = w
-    turn = one_hot_swap(col_tok, seqs)
-    turn_ref[...] = turn
+    turn = turn_ref[...]
     xn = normed(x_ref[...].astype(F32).reshape(seqs * col_tok, feat)).astype(BF16)
     xn_ref[...] = xn.reshape(xn_ref.shape)
     proj_ref[...] = mm(mm(turn, xn).astype(BF16), w)
@@ -148,11 +151,10 @@
     right = got[:, row_tok * width :]
     gran = lane_iota((row_tok, 128)) // width
     group = per * row_tok
-    delta = None
+    halves = []
     for pair in range(0, width // per, 2):
         outer = mm(left[:, pair * group : (pair + 2) * group], right, ((0,), (0,)))
         outer = (outer * inv).astype(BF16)
-        halves = []
         for half in range(2):
             tiles = []
             for jh in range(col_tok // per):
@@ -172,8 +174,7 @@
                     step *= 2
                 tiles += a
             halves.append(jnp.concatenate(tiles, axis=0))
-        part = mm(jnp.concatenate(halves, axis=1), mean_ref[pair * 128 : (pair + 2) * 128, :])
-        delta = part if delta is None else delta + part
+    delta = mm(jnp.concatenate(halves, axis=1), mean_ref[...])
     return (state.astype(F32) + delta).astype(BF16)
 
 
@@ -297,13 +298,14 @@
     xs = [lax.ppermute(x, "col", [(i, (i + k) % cols) for i in range(cols)]) for k in range(1, cols)]
     other_pair = lax.ppermute(pair, ("row", "col"), swap)
 
-    own, proj, w, turn, token, seq, inv = call(
+    (turn,) = call(turn_kernel, [((mine, mine), BF16)], [], flops=20_000_000_000, seqs=seqs, col_tok=col_tok)
+    own, proj, w, token, seq, inv = call(
         own_kernel,
         [
-            (x.shape, BF16), ((mine, 256), F32), ((feat, 256), BF16), ((mine, mine), BF16),
+            (x.shape, BF16), ((mine, 256), F32), ((feat, 256), BF16),
             ((tokens * width // 128, 128), F32), ((seqs, 128), F32), ((8, 128), F32),
         ],
-        [x, wp, present.reshape(1, -1), live.reshape(1, -1)],
+        [x, wp, present.reshape(1, -1), live.reshape(1, -1), turn],
         flops=30_000_000, width=width,
     )
     send, xn = call(

time: 46.3 us -> 45.6 us (0.985)
  waiting for transfers between devices: 9.22 us -> 11.6 us
  local copies, waits for them, and re-layouts: 2.93 us -> 1.34 us
  Pallas kernels: 10.5 us -> 9.08 us
    unnamed x26 -> x24, local copies, waits for them, and re-layouts: 2.93 us -> 1.34 us
    ppermute x3, waiting for transfers between devices: 2.92 us -> 4.44 us  [body(): lax.ppermute(x, 'col', [(i, (i + k) % cols) for i in range(cols)])]
    pallas_call x7 -> x8, Pallas kernels: 10.5 us -> 9.08 us  [call(): pl.pallas_call(functools.partial(kernel, **keys), out_shape=tuple((jax.Sh...]
    all_to_all x1, waiting for transfers between devices: 1.7 us -> 2.57 us  [body(): scores = lax.all_to_all(chunk, 'row', 0, 0)]
  transfers between devices with their start and end apart: 6 -> 6, of which waited for: 3 -> 4; matrix products, arithmetic and copies ran while one was open for 0% -> 0% of each run, Pallas kernels for 10% -> 9%
where the time goes in v1:
time: 45.6 us; the launch traced here: 45.2 us
  starting transfers between devices  22.4 us (49%)
  waiting for transfers between devices  11.6 us (25%)
  Pallas kernels  9.08 us (20%)
  local copies, waits for them, and re-layouts  1.34 us (3%)
  between operations  0.79 us (2%)
    pallas_call x8, Pallas kernels, call(): pl.pallas_call(functools.partial(kernel, **keys), out_shape=tuple((jax.Sh...  9.08 us
    all_to_all x1, starting transfers between devices, body(): scores = lax.all_to_all(chunk, 'row', 0, 0)  7.56 us
    ppermute x3, starting transfers between devices, body(): lax.ppermute(x, 'col', [(i, (i + k) % cols) for i in range(cols)])  6.14 us
    ppermute x1, starting transfers between devices, body(): other_pair = lax.ppermute(pair, ('row', 'col'), swap)  4.82 us
    ppermute x1, waiting for transfers between devices, body(): other_pair = lax.ppermute(pair, ('row', 'col'), swap)  4.59 us
    ppermute x3, waiting for transfers between devices, body(): lax.ppermute(x, 'col', [(i, (i + k) % cols) for i in range(cols)])  4.44 us
    all_to_all x1, starting transfers between devices, body(): got = lax.all_to_all(send, 'row', 0, 0)  3.86 us
    all_to_all x1, waiting for transfers between devices, body(): scores = lax.all_to_all(chunk, 'row', 0, 0)  2.57 us
  transfers between devices with their start and end apart: 6, of which 4 were waited for; matrix products, arithmetic and copies ran while one was open for 0% of the time, Pallas kernels for 9%

profile of v1, /device:TPU:0, one launch (start us, length us, event | category | flops | bytes accessed | tf_op | source)
XLA Modules:
  0.0 45.2 jit_solution(11584741705781040587)
XLA Ops:
  0.6 0.0 copy-start.1
  0.6 0.0 copy-start.5
  0.6 5.1 %collective-permute-start.2 = (bf16[8,32,64]{2,1,0:T(8,128)(2,1)}, bf16[8,32,64]{2,1,0:T(8,128)(2,1)S(1)}, u32[]{:S(2)}, u32[]{:S(2)}) collective-permute-start(bf16[8,32,64]{2,1,0:T(8,128)(2,1)} %x_ref.3), channel_id=1, source_target_pairs={{0,3},{1,0},{2,1},{3,2},{4,7},{5,4},{6,5},{7,6},{8,11},{9,8},{10,9... | collective-permute-start | bytes 98312 | tf_op jit(solution)/shard_map/ppermute | solution.py:298
  5.8 0.0 collective-permute-start.1
  5.8 1.0 %collective-permute-start = (bf16[8,32,64]{2,1,0:T(8,128)(2,1)}, bf16[8,32,64]{2,1,0:T(8,128)(2,1)S(1)}, u32[]{:S(2)}, u32[]{:S(2)}) collective-permute-start(bf16[8,32,64]{2,1,0:T(8,128)(2,1)} %x_ref.3), channel_id=1, source_target_pairs={{0,1},{1,2},{2,3},{3,0},{4,5},{5,6},{6,7},{7,4},{8,9},{9,10},{10,1... | collective-permute-start | bytes 98312 | tf_op jit(solution)/shard_map/ppermute | solution.py:298
  6.8 0.0 copy-start.7
  6.9 0.0 copy-start.8
  6.9 0.0 copy-done.1
  6.9 0.0 copy-done.5
  6.9 0.6 %copy-done.7 = s32[128]{0:T(128)S(1)} copy-done((s32[128]{0:T(128)S(1)}, s32[128]{0:T(128)}, u32[]{:S(2)}) %copy-start.7) | copy-done | bytes 536
  7.5 0.0 copy-done.8
  7.5 0.5 %shard_map.132 = (bf16[8,32,64]{2,1,0:T(8,128)(2,1)S(1)}, f32[256,256]{1,0:T(8,128)S(1)}, bf16[64,256]{1,0:T(8,128)(2,1)S(1)}, f32[32,128]{1,0:T(8,128)S(1)}, f3...) custom-call(bf16[8,32,64]{2,1,0:T(8,128)(2,1)S(1)} %copy-done.1, bf16[64,64]{1,0:T(8,128)(2,1)S(1)} %copy-done.5, ...), custom_call_target="tpu_custom_call" | custom-call | flops 30000000 | tf_op jit(solution)/shard_map/pallas_call | solution.py:266
  8.0 0.6 %collective-permute-done.2.refs_2_ = bf16[8,32,64]{2,1,0:T(8,128)(2,1)S(1)} collective-permute-done((bf16[8,32,64]{2,1,0:T(8,128)(2,1)}, bf16[8,32,64]{2,1,0:T(8,128)(2,1)S(1)}, u32[]{:S(2)}, u32[]{:S(2)}) %collective-permute-start.2) | collective-permute-done | bytes 32800 | tf_op jit(solution)/shard_map/ppermute | solution.py:298
  8.6 3.9 %collective-permute-done.1.refs_1_ = bf16[8,32,64]{2,1,0:T(8,128)(2,1)S(1)} collective-permute-done((bf16[8,32,64]{2,1,0:T(8,128)(2,1)}, bf16[8,32,64]{2,1,0:T(8,128)(2,1)S(1)}, u32[]{:S(2)}, u32[]{:S(2)}) %collective-permute-start.1) | collective-permute-done | bytes 32800 | tf_op jit(solution)/shard_map/ppermute | solution.py:298
  12.5 0.0 collective-permute-done.refs_0_
  12.5 1.5 %shard_map.133 = (bf16[8,8,3072]{2,1,0:T(8,128)(2,1)}, bf16[4,8,32,64]{3,2,1,0:T(8,128)(2,1)S(1)}) custom-call(bf16[8,32,64]{2,1,0:T(8,128)(2,1)S(1)} %collective-permute-done.refs_0_, bf16[8,32,64]{2,1,0:T(8,128)(2,1)S(1)} %collective-permute-done.1.refs_1_, bf16[8,32,64]{2,1,0:T(8,128)(2,1)S(1)} %collective-permute-done.2.refs_2_, ...), custom_call_target="tpu_custom_call" | custom-call | tf_op jit(solution)/shard_map/pallas_call | solution.py:266
  14.0 3.9 %all-to-all-start = ((bf16[8,8,3072]{2,1,0:T(8,128)(2,1)}), bf16[8,8,3072]{2,1,0:T(8,128)(2,1)S(1)}, u32[]{:S(2)}, u32[]{:S(2)}) async-start(bf16[8,8,3072]{2,1,0:T(8,128)(2,1)} %get-tuple-element.20), calls=%async_computation | async-start | bytes 786432 | tf_op jit(solution)/shard_map/all_to_all | solution.py:317
  17.9 4.8 %collective-permute-start.3 = (bf16[16,32,128]{2,1,0:T(8,128)(2,1)S(1)}, bf16[16,32,128]{2,1,0:T(8,128)(2,1)S(1)}, u32[]{:S(2)}, u32[]{:S(2)}) collective-permute-start(bf16[16,32,128]{2,1,0:T(8,128)(2,1)S(1)} %copy-done.10), channel_id=1, source_target_pairs={{0,24},{1,16},{2,8},{3,0},{4,28},{5,20},{6,12},{7,4},{8,17},{9,25}... | collective-permute-start | bytes 393224 | tf_op jit(solution)/shard_map/ppermute | solution.py:299
  22.7 0.3 shard_map.136
  23.0 0.0 copy-start
  23.1 4.6 %collective-permute-done.3.other_ref = bf16[16,32,128]{2,1,0:T(8,128)(2,1)S(1)} collective-permute-done((bf16[16,32,128]{2,1,0:T(8,128)(2,1)S(1)}, bf16[16,32,128]{2,1,0:T(8,128)(2,1)S(1)}, u32[]{:S(2)}, u32[]{:S(2)}) %collective-permute-start.3) | collective-permute-done | bytes 131104 | tf_op jit(solution)/shard_map/ppermute | solution.py:299
  27.6 0.5 %shard_map.134 = (bf16[512,512]{1,0:T(8,128)(2,1)S(1)}, bf16[512,128]{1,0:T(8,128)(2,1)S(1)}, bf16[512,128]{1,0:T(8,128)(2,1)S(1)}) custom-call(bf16[16,32,128]{2,1,0:T(8,128)(2,1)S(1)} %copy-done.10, bf16[16,32,128]{2,1,0:T(8,128)(2,1)S(1)} %collective-permute-done.3.other_ref), custom_call_target="tpu_custom_call" | custom-call | flops 100000000 | tf_op jit(solution)/shard_map/pallas_call | solution.py:266
  28.1 0.0 copy-start.6
  28.1 0.0 all-to-all-done.got_ref
  28.2 0.0 copy-done
  28.2 0.7 %copy-done.6 = f32[128,8]{0,1:T(8,128)S(1)} copy-done((f32[128,8]{0,1:T(8,128)S(1)}, f32[128,8]{0,1:T(8,128)}, u32[]{:S(2)}) %copy-start.6) | copy-done | bytes 4120
  28.8 2.4 %shard_map.135 = bf16[8,40,128]{2,1,0:T(8,128)(2,1)} custom-call(bf16[8,8,3072]{2,1,0:T(8,128)(2,1)S(1)} %all-to-all-done.got_ref, bf16[512,128]{1,0:T(8,128)(2,1)S(1)} %get-tuple-element.21.state_ref, bf16[1024,128]{1,0:T(8,128)(2,1)S(1)} %copy-done, bf16[512,512]{1,0:T(8,128)(2,1)S(1)} %get-tuple-element.22.swap_ref, f32[8,128]{1,0:T(8,128)S(1)} %bitcast.5, ...), custom_call_target="tpu_custom_call" | custom-call | tf_op jit(solution)/shard_map/pallas_call | solution.py:266
  31.2 7.6 %all-to-all-start.1 = ((bf16[8,40,128]{2,1,0:T(8,128)(2,1)}), bf16[8,40,128]{2,1,0:T(8,128)(2,1)S(1)}, u32[]{:S(2)}, u32[]{:S(2)}) async-start(bf16[8,40,128]{2,1,0:T(8,128)(2,1)} %shard_map.135), calls=%async_computation.1 | async-start | bytes 163840 | tf_op jit(solution)/shard_map/all_to_all | solution.py:335
  38.8 0.0 copy-start.4
  38.8 2.5 %shard_map.137.pair_ref = bf16[16,32,128]{2,1,0:T(8,128)(2,1)S(1)} custom-call(bf16[8,8,3072]{2,1,0:T(8,128)(2,1)S(1)} %all-to-all-done.got_ref, bf16[512,128]{1,0:T(8,128)(2,1)S(1)} %get-tuple-element.27.state_ref, bf16[1024,128]{1,0:T(8,128)(2,1)S(1)} %copy-done, bf16[512,512]{1,0:T(8,128)(2,1)S(1)} %get-tuple-element.22.swap_ref, ...), custom_call_target="tpu_custom_call" | custom-call | flops 1000000000 | tf_op jit(solution)/shard_map/pallas_call | solution.py:266
  41.3 2.6 %all-to-all-done.1.got_ref = bf16[8,40,128]{2,1,0:T(8,128)(2,1)S(1)} async-done(((bf16[8,40,128]{2,1,0:T(8,128)(2,1)}), bf16[8,40,128]{2,1,0:T(8,128)(2,1)S(1)}, u32[]{:S(2)}, u32[]{:S(2)}) %all-to-all-start.1) | async-done | bytes 81952 | tf_op jit(solution)/shard_map/all_to_all | solution.py:335
  43.9 1.3 %shard_map.138 = (bf16[8,32,64]{2,1,0:T(8,128)(2,1)}, bf16[16,32,128]{2,1,0:T(8,128)(2,1)}) custom-call(bf16[8,40,128]{2,1,0:T(8,128)(2,1)S(1)} %all-to-all-done.1.got_ref, bf16[8,128,256]{2,1,0:T(8,128)(2,1)S(1)} %get-tuple-element.25.values_ref, f32[256,256]{1,0:T(8,128)S(1)} %get-tuple-element.26.gate_ref, bf16[8,32,64]{2,1,0:T(8,128)(2,1)S(1)} %copy-done.1, ...), custom_call_target="tpu_custom_call" | custom-call | tf_op jit(solution)/shard_map/pallas_call | solution.py:266
  (12 shorter events, 0.1 us)
Async XLA Ops:
  0.6 6.2 %copy-start.1 = (bf16[8,32,64]{2,1,0:T(8,128)(2,1)S(1)}, bf16[8,32,64]{2,1,0:T(8,128)(2,1)}, u32[]{:S(2)}) copy-start(bf16[8,32,64]{2,1,0:T(8,128)(2,1)} %x_ref.3) | copy-start | bytes 98308
  0.6 6.2 %copy-start.5 = (bf16[64,64]{1,0:T(8,128)(2,1)S(1)}, bf16[64,64]{1,0:T(8,128)(2,1)}, u32[]{:S(2)}) copy-start(bf16[64,64]{1,0:T(8,128)(2,1)} %wp_ref.1) | copy-start | bytes 24580
  0.6 7.9 %collective-permute-start.2 = (bf16[8,32,64]{2,1,0:T(8,128)(2,1)}, bf16[8,32,64]{2,1,0:T(8,128)(2,1)S(1)}, u32[]{:S(2)}, u32[]{:S(2)}) collective-permute-start(bf16[8,32,64]{2,1,0:T(8,128)(2,1)} %x_ref.3), channel_id=1, source_target_pairs={{0,3},{1,0},{2,1},{3,2},{4,7},{5,4},{6,5},{7,6},{8,11},{9,8},{10,9... | collective-permute-start | bytes 98312 | tf_op jit(solution)/shard_map/ppermute | solution.py:298
  5.8 6.7 %collective-permute-start.1 = (bf16[8,32,64]{2,1,0:T(8,128)(2,1)}, bf16[8,32,64]{2,1,0:T(8,128)(2,1)S(1)}, u32[]{:S(2)}, u32[]{:S(2)}) collective-permute-start(bf16[8,32,64]{2,1,0:T(8,128)(2,1)} %x_ref.3), channel_id=1, source_target_pairs={{0,2},{1,3},{2,0},{3,1},{4,6},{5,7},{6,4},{7,5},{8,10},{9,11},{10,... | collective-permute-start | bytes 98312 | tf_op jit(solution)/shard_map/ppermute | solution.py:298
  5.8 6.7 %collective-permute-start = (bf16[8,32,64]{2,1,0:T(8,128)(2,1)}, bf16[8,32,64]{2,1,0:T(8,128)(2,1)S(1)}, u32[]{:S(2)}, u32[]{:S(2)}) collective-permute-start(bf16[8,32,64]{2,1,0:T(8,128)(2,1)} %x_ref.3), channel_id=1, source_target_pairs={{0,1},{1,2},{2,3},{3,0},{4,5},{5,6},{6,7},{7,4},{8,9},{9,10},{10,1... | collective-permute-start | bytes 98312 | tf_op jit(solution)/shard_map/ppermute | solution.py:298
  6.8 0.7 %copy-start.7 = (s32[128]{0:T(128)S(1)}, s32[128]{0:T(128)}, u32[]{:S(2)}) copy-start(s32[128]{0:T(128)} %param.15) | copy-start | bytes 1540
  6.9 0.7 %copy-start.8 = (s32[64]{0:T(128)S(1)}, s32[64]{0:T(128)}, u32[]{:S(2)}) copy-start(s32[64]{0:T(128)} %param.14) | copy-start | bytes 772
  14.0 3.9 %copy-start.10 = (bf16[16,32,128]{2,1,0:T(8,128)(2,1)S(1)}, bf16[16,32,128]{2,1,0:T(8,128)(2,1)}, u32[]{:S(2)}) copy-start(bf16[16,32,128]{2,1,0:T(8,128)(2,1)} %pair_ref.1) | copy-start | bytes 393220
  14.0 8.7 %copy-start.2 = (bf16[64,256]{1,0:T(8,128)(2,1)S(1)}, bf16[64,256]{1,0:T(8,128)(2,1)}, u32[]{:S(2)}) copy-start(bf16[64,256]{1,0:T(8,128)(2,1)} %wv_ref.1) | copy-start | bytes 98308
  14.0 8.7 %copy-start.3 = (bf16[64,256]{1,0:T(8,128)(2,1)S(1)}, bf16[64,256]{1,0:T(8,128)(2,1)}, u32[]{:S(2)}) copy-start(bf16[64,256]{1,0:T(8,128)(2,1)} %wg_ref.1) | copy-start | bytes 98308
  14.0 14.1 %all-to-all-start = ((bf16[8,8,3072]{2,1,0:T(8,128)(2,1)}), bf16[8,8,3072]{2,1,0:T(8,128)(2,1)S(1)}, u32[]{:S(2)}, u32[]{:S(2)}) async-start(bf16[8,8,3072]{2,1,0:T(8,128)(2,1)} %get-tuple-element.20), calls=%async_computation | async-start | bytes 786432 | tf_op jit(solution)/shard_map/all_to_all | solution.py:317
  17.9 9.8 %collective-permute-start.3 = (bf16[16,32,128]{2,1,0:T(8,128)(2,1)S(1)}, bf16[16,32,128]{2,1,0:T(8,128)(2,1)S(1)}, u32[]{:S(2)}, u32[]{:S(2)}) collective-permute-start(bf16[16,32,128]{2,1,0:T(8,128)(2,1)S(1)} %copy-done.10), channel_id=1, source_target_pairs={{0,24},{1,16},{2,8},{3,0},{4,28},{5,20},{6,12},{7,4},{8,17},{9,25}... | collective-permute-start | bytes 393224 | tf_op jit(solution)/shard_map/ppermute | solution.py:299
  23.0 5.1 %copy-start = (bf16[1024,128]{1,0:T(8,128)(2,1)S(1)}, bf16[1024,128]{1,0:T(8,128)(2,1)}, u32[]{:S(2)}) copy-start(bf16[1024,128]{1,0:T(8,128)(2,1)} %mean_ref.3) | copy-start | bytes 786436
  28.1 0.7 %copy-start.6 = (f32[128,8]{0,1:T(8,128)S(1)}, f32[128,8]{0,1:T(8,128)}, u32[]{:S(2)}) copy-start(f32[128,8]{0,1:T(8,128)} %param.18) | copy-start | bytes 12292
  28.8 9.9 %copy-start.9 = (bf16[128,1024]{1,0:T(8,128)(2,1)S(1)}, bf16[128,1024]{1,0:T(8,128)(2,1)}, u32[]{:S(2)}) copy-start(bf16[128,1024]{1,0:T(8,128)(2,1)} %win_ref.1) | copy-start | bytes 786436
  31.2 7.6 %copy-start.11 = (bf16[512,128]{1,0:T(8,128)(2,1)S(1)}, bf16[512,128]{1,0:T(8,128)(2,1)}, u32[]{:S(2)}) copy-start(bf16[512,128]{1,0:T(8,128)(2,1)} %wout_ref.1) | copy-start | bytes 393220
  31.2 12.7 %all-to-all-start.1 = ((bf16[8,40,128]{2,1,0:T(8,128)(2,1)}), bf16[8,40,128]{2,1,0:T(8,128)(2,1)S(1)}, u32[]{:S(2)}, u32[]{:S(2)}) async-start(bf16[8,40,128]{2,1,0:T(8,128)(2,1)} %shard_map.135), calls=%async_computation.1 | async-start | bytes 163840 | tf_op jit(solution)/shard_map/all_to_all | solution.py:335
  38.8 5.1 %copy-start.4 = (bf16[256,64]{0,1:T(8,128)(2,1)S(1)}, bf16[256,64]{0,1:T(8,128)(2,1)}, u32[]{:S(2)}) copy-start(bf16[256,64]{0,1:T(8,128)(2,1)} %param.21) | copy-start | bytes 98308

commit v2 on v1

--- a/solution.py
+++ b/solution.py
@@ -58,12 +58,12 @@
     xn = normed(x_ref[...].astype(F32).reshape(seqs * col_tok, feat)).astype(BF16)
     xn_ref[...] = xn.reshape(xn_ref.shape)
     proj_ref[...] = mm(mm(turn, xn).astype(BF16), w)
-    flags = present_ref[...].astype(F32)
+    flags = present_ref[...].astype(F32).reshape(1, -1)
     shape = (seqs, flags.shape[1])
     mine = lane_iota(shape) == row * seqs + lax.broadcasted_iota(jnp.int32, shape, 0)
     own_flags = jnp.sum(jnp.where(mine, flags, 0.0), axis=1, keepdims=True)
     seq_ref[...] = jnp.broadcast_to(own_flags, seq_ref.shape)
-    live = live_ref[...].astype(F32)
+    live = live_ref[...].astype(F32).reshape(1, -1)
     tokens = live.shape[1]
     shape = (token_ref.shape[0], tokens)
     here = lane_iota(shape) // per == lax.broadcasted_iota(jnp.int32, shape, 0)
@@ -305,7 +305,7 @@
             (x.shape, BF16), ((mine, 256), F32), ((feat, 256), BF16),
             ((tokens * width // 128, 128), F32), ((seqs, 128), F32), ((8, 128), F32),
         ],
-        [x, wp, present.reshape(1, -1), live.reshape(1, -1), turn],
+        [x, wp, present, live, turn],
         flops=30_000_000, width=width,
     )
     send, xn = call(

time: 45.6 us -> 45.6 us (level)
  local copies, waits for them, and re-layouts: 1.34 us -> 0.71 us
  waiting for transfers between devices: 11.6 us -> 12.2 us
    ppermute x3, waiting for transfers between devices: 4.44 us -> 5.07 us  [body(): lax.ppermute(x, 'col', [(i, (i + k) % cols) for i in range(cols)])]
    unnamed x24, local copies, waits for them, and re-layouts: 1.34 us -> 0.71 us
where the time goes in v2:
time: 45.6 us; the launch traced here: 45.2 us
  starting transfers between devices  22.4 us (49%)
  waiting for transfers between devices  12.2 us (27%)
  Pallas kernels  9.09 us (20%)
  between operations  0.81 us (2%)
  local copies, waits for them, and re-layouts  0.71 us (2%)
    pallas_call x8, Pallas kernels, call(): pl.pallas_call(functools.partial(kernel, **keys), out_shape=tuple((jax.Sh...  9.09 us
    all_to_all x1, starting transfers between devices, body(): scores = lax.all_to_all(chunk, 'row', 0, 0)  7.56 us
    ppermute x3, starting transfers between devices, body(): lax.ppermute(x, 'col', [(i, (i + k) % cols) for i in range(cols)])  6.14 us
    ppermute x3, waiting for transfers between devices, body(): lax.ppermute(x, 'col', [(i, (i + k) % cols) for i in range(cols)])  5.07 us
    ppermute x1, starting transfers between devices, body(): other_pair = lax.ppermute(pair, ('row', 'col'), swap)  4.82 us
    ppermute x1, waiting for transfers between devices, body(): other_pair = lax.ppermute(pair, ('row', 'col'), swap)  4.59 us
    all_to_all x1, starting transfers between devices, body(): got = lax.all_to_all(send, 'row', 0, 0)  3.85 us
    all_to_all x1, waiting for transfers between devices, body(): scores = lax.all_to_all(chunk, 'row', 0, 0)  2.57 us
  transfers between devices with their start and end apart: 6, of which 4 were waited for; matrix products, arithmetic and copies ran while one was open for 0% of the time, Pallas kernels for 9%

profile of v2, /device:TPU:0, one launch (start us, length us, event | category | flops | bytes accessed | tf_op | source)
XLA Modules:
  0.0 45.2 jit_solution(337111383013224565)
XLA Ops:
  0.6 0.0 copy-start.1
  0.6 0.0 copy-start.7
  0.7 0.0 copy-start.5
  0.7 0.0 copy-start.8
  0.7 5.1 %collective-permute-start.2 = (bf16[8,32,64]{2,1,0:T(8,128)(2,1)}, bf16[8,32,64]{2,1,0:T(8,128)(2,1)S(1)}, u32[]{:S(2)}, u32[]{:S(2)}) collective-permute-start(bf16[8,32,64]{2,1,0:T(8,128)(2,1)} %x_ref.3), channel_id=1, source_target_pairs={{0,3},{1,0},{2,1},{3,2},{4,7},{5,4},{6,5},{7,6},{8,11},{9,8},{10,9... | collective-permute-start | bytes 98312 | tf_op jit(solution)/shard_map/ppermute | solution.py:298
  5.8 0.0 collective-permute-start.1
  5.8 1.0 %collective-permute-start = (bf16[8,32,64]{2,1,0:T(8,128)(2,1)}, bf16[8,32,64]{2,1,0:T(8,128)(2,1)S(1)}, u32[]{:S(2)}, u32[]{:S(2)}) collective-permute-start(bf16[8,32,64]{2,1,0:T(8,128)(2,1)} %x_ref.3), channel_id=1, source_target_pairs={{0,1},{1,2},{2,3},{3,0},{4,5},{5,6},{6,7},{7,4},{8,9},{9,10},{10,1... | collective-permute-start | bytes 98312 | tf_op jit(solution)/shard_map/ppermute | solution.py:298
  6.9 0.0 copy-done.1
  6.9 0.0 copy-done.7
  6.9 0.0 copy-done.5
  6.9 0.0 copy-done.8
  6.9 0.5 %shard_map.132 = (bf16[8,32,64]{2,1,0:T(8,128)(2,1)S(1)}, f32[256,256]{1,0:T(8,128)S(1)}, bf16[64,256]{1,0:T(8,128)(2,1)S(1)}, f32[32,128]{1,0:T(8,128)S(1)}, f3...) custom-call(bf16[8,32,64]{2,1,0:T(8,128)(2,1)S(1)} %copy-done.1, bf16[64,64]{1,0:T(8,128)(2,1)S(1)} %copy-done.5, ...), custom_call_target="tpu_custom_call" | custom-call | flops 30000000 | tf_op jit(solution)/shard_map/pallas_call | solution.py:266
  7.4 1.2 %collective-permute-done.2.refs_2_ = bf16[8,32,64]{2,1,0:T(8,128)(2,1)S(1)} collective-permute-done((bf16[8,32,64]{2,1,0:T(8,128)(2,1)}, bf16[8,32,64]{2,1,0:T(8,128)(2,1)S(1)}, u32[]{:S(2)}, u32[]{:S(2)}) %collective-permute-start.2) | collective-permute-done | bytes 32800 | tf_op jit(solution)/shard_map/ppermute | solution.py:298
  8.6 3.9 %collective-permute-done.1.refs_1_ = bf16[8,32,64]{2,1,0:T(8,128)(2,1)S(1)} collective-permute-done((bf16[8,32,64]{2,1,0:T(8,128)(2,1)}, bf16[8,32,64]{2,1,0:T(8,128)(2,1)S(1)}, u32[]{:S(2)}, u32[]{:S(2)}) %collective-permute-start.1) | collective-permute-done | bytes 32800 | tf_op jit(solution)/shard_map/ppermute | solution.py:298
  12.5 0.0 collective-permute-done.refs_0_
  12.5 1.5 %shard_map.133 = (bf16[8,8,3072]{2,1,0:T(8,128)(2,1)}, bf16[4,8,32,64]{3,2,1,0:T(8,128)(2,1)S(1)}) custom-call(bf16[8,32,64]{2,1,0:T(8,128)(2,1)S(1)} %collective-permute-done.refs_0_, bf16[8,32,64]{2,1,0:T(8,128)(2,1)S(1)} %collective-permute-done.1.refs_1_, bf16[8,32,64]{2,1,0:T(8,128)(2,1)S(1)} %collective-permute-done.2.refs_2_, ...), custom_call_target="tpu_custom_call" | custom-call | tf_op jit(solution)/shard_map/pallas_call | solution.py:266
  14.0 3.9 %all-to-all-start = ((bf16[8,8,3072]{2,1,0:T(8,128)(2,1)}), bf16[8,8,3072]{2,1,0:T(8,128)(2,1)S(1)}, u32[]{:S(2)}, u32[]{:S(2)}) async-start(bf16[8,8,3072]{2,1,0:T(8,128)(2,1)} %get-tuple-element.20), calls=%async_computation | async-start | bytes 786432 | tf_op jit(solution)/shard_map/all_to_all | solution.py:317
  17.9 0.0 copy-done.10
  17.9 4.8 %collective-permute-start.3 = (bf16[16,32,128]{2,1,0:T(8,128)(2,1)S(1)}, bf16[16,32,128]{2,1,0:T(8,128)(2,1)S(1)}, u32[]{:S(2)}, u32[]{:S(2)}) collective-permute-start(bf16[16,32,128]{2,1,0:T(8,128)(2,1)S(1)} %copy-done.10), channel_id=1, source_target_pairs={{0,24},{1,16},{2,8},{3,0},{4,28},{5,20},{6,12},{7,4},{8,17},{9,25}... | collective-permute-start | bytes 393224 | tf_op jit(solution)/shard_map/ppermute | solution.py:299
  22.7 0.3 shard_map.136
  23.1 0.0 copy-start
  23.1 4.6 %collective-permute-done.3.other_ref = bf16[16,32,128]{2,1,0:T(8,128)(2,1)S(1)} collective-permute-done((bf16[16,32,128]{2,1,0:T(8,128)(2,1)S(1)}, bf16[16,32,128]{2,1,0:T(8,128)(2,1)S(1)}, u32[]{:S(2)}, u32[]{:S(2)}) %collective-permute-start.3) | collective-permute-done | bytes 131104 | tf_op jit(solution)/shard_map/ppermute | solution.py:299
  27.7 0.5 %shard_map.134 = (bf16[512,512]{1,0:T(8,128)(2,1)S(1)}, bf16[512,128]{1,0:T(8,128)(2,1)S(1)}, bf16[512,128]{1,0:T(8,128)(2,1)S(1)}) custom-call(bf16[16,32,128]{2,1,0:T(8,128)(2,1)S(1)} %copy-done.10, bf16[16,32,128]{2,1,0:T(8,128)(2,1)S(1)} %collective-permute-done.3.other_ref), custom_call_target="tpu_custom_call" | custom-call | flops 100000000 | tf_op jit(solution)/shard_map/pallas_call | solution.py:266
  28.2 0.0 copy-start.6
  28.2 0.0 all-to-all-done.got_ref
  28.2 0.7 %copy-done.6 = f32[128,8]{0,1:T(8,128)S(1)} copy-done((f32[128,8]{0,1:T(8,128)S(1)}, f32[128,8]{0,1:T(8,128)}, u32[]{:S(2)}) %copy-start.6) | copy-done | bytes 4120
  28.8 2.4 %shard_map.135 = bf16[8,40,128]{2,1,0:T(8,128)(2,1)} custom-call(bf16[8,8,3072]{2,1,0:T(8,128)(2,1)S(1)} %all-to-all-done.got_ref, bf16[512,128]{1,0:T(8,128)(2,1)S(1)} %get-tuple-element.21.state_ref, bf16[1024,128]{1,0:T(8,128)(2,1)S(1)} %copy-done, bf16[512,512]{1,0:T(8,128)(2,1)S(1)} %get-tuple-element.22.swap_ref, f32[8,128]{1,0:T(8,128)S(1)} %bitcast.4, ...), custom_call_target="tpu_custom_call" | custom-call | tf_op jit(solution)/shard_map/pallas_call | solution.py:266
  31.2 7.6 %all-to-all-start.1 = ((bf16[8,40,128]{2,1,0:T(8,128)(2,1)}), bf16[8,40,128]{2,1,0:T(8,128)(2,1)S(1)}, u32[]{:S(2)}, u32[]{:S(2)}) async-start(bf16[8,40,128]{2,1,0:T(8,128)(2,1)} %shard_map.135), calls=%async_computation.1 | async-start | bytes 163840 | tf_op jit(solution)/shard_map/all_to_all | solution.py:335
  38.8 0.0 copy-start.4
  38.8 2.5 %shard_map.137.pair_ref = bf16[16,32,128]{2,1,0:T(8,128)(2,1)S(1)} custom-call(bf16[8,8,3072]{2,1,0:T(8,128)(2,1)S(1)} %all-to-all-done.got_ref, bf16[512,128]{1,0:T(8,128)(2,1)S(1)} %get-tuple-element.27.state_ref, bf16[1024,128]{1,0:T(8,128)(2,1)S(1)} %copy-done, bf16[512,512]{1,0:T(8,128)(2,1)S(1)} %get-tuple-element.22.swap_ref, ...), custom_call_target="tpu_custom_call" | custom-call | flops 1000000000 | tf_op jit(solution)/shard_map/pallas_call | solution.py:266
  41.3 2.6 %all-to-all-done.1.got_ref = bf16[8,40,128]{2,1,0:T(8,128)(2,1)S(1)} async-done(((bf16[8,40,128]{2,1,0:T(8,128)(2,1)}), bf16[8,40,128]{2,1,0:T(8,128)(2,1)S(1)}, u32[]{:S(2)}, u32[]{:S(2)}) %all-to-all-start.1) | async-done | bytes 81952 | tf_op jit(solution)/shard_map/all_to_all | solution.py:335
  43.9 1.3 %shard_map.138 = (bf16[8,32,64]{2,1,0:T(8,128)(2,1)}, bf16[16,32,128]{2,1,0:T(8,128)(2,1)}) custom-call(bf16[8,40,128]{2,1,0:T(8,128)(2,1)S(1)} %all-to-all-done.1.got_ref, bf16[8,128,256]{2,1,0:T(8,128)(2,1)S(1)} %get-tuple-element.25.values_ref, f32[256,256]{1,0:T(8,128)S(1)} %get-tuple-element.26.gate_ref, bf16[8,32,64]{2,1,0:T(8,128)(2,1)S(1)} %copy-done.1, ...), custom_call_target="tpu_custom_call" | custom-call | tf_op jit(solution)/shard_map/pallas_call | solution.py:266
  (12 shorter events, 0.1 us)
Async XLA Ops:
  0.6 6.2 %copy-start.1 = (bf16[8,32,64]{2,1,0:T(8,128)(2,1)S(1)}, bf16[8,32,64]{2,1,0:T(8,128)(2,1)}, u32[]{:S(2)}) copy-start(bf16[8,32,64]{2,1,0:T(8,128)(2,1)} %x_ref.3) | copy-start | bytes 98308
  0.6 6.2 %copy-start.7 = (s32[128]{0:T(128)S(1)}, s32[128]{0:T(128)}, u32[]{:S(2)}) copy-start(s32[128]{0:T(128)} %live_ref.1) | copy-start | bytes 1540
  0.7 6.2 %copy-start.5 = (bf16[64,64]{1,0:T(8,128)(2,1)S(1)}, bf16[64,64]{1,0:T(8,128)(2,1)}, u32[]{:S(2)}) copy-start(bf16[64,64]{1,0:T(8,128)(2,1)} %wp_ref.1) | copy-start | bytes 24580
  0.7 6.2 %copy-start.8 = (s32[64]{0:T(128)S(1)}, s32[64]{0:T(128)}, u32[]{:S(2)}) copy-start(s32[64]{0:T(128)} %present_ref.1) | copy-start | bytes 772
  0.7 7.9 %collective-permute-start.2 = (bf16[8,32,64]{2,1,0:T(8,128)(2,1)}, bf16[8,32,64]{2,1,0:T(8,128)(2,1)S(1)}, u32[]{:S(2)}, u32[]{:S(2)}) collective-permute-start(bf16[8,32,64]{2,1,0:T(8,128)(2,1)} %x_ref.3), channel_id=1, source_target_pairs={{0,3},{1,0},{2,1},{3,2},{4,7},{5,4},{6,5},{7,6},{8,11},{9,8},{10,9... | collective-permute-start | bytes 98312 | tf_op jit(solution)/shard_map/ppermute | solution.py:298
  5.8 6.7 %collective-permute-start.1 = (bf16[8,32,64]{2,1,0:T(8,128)(2,1)}, bf16[8,32,64]{2,1,0:T(8,128)(2,1)S(1)}, u32[]{:S(2)}, u32[]{:S(2)}) collective-permute-start(bf16[8,32,64]{2,1,0:T(8,128)(2,1)} %x_ref.3), channel_id=1, source_target_pairs={{0,2},{1,3},{2,0},{3,1},{4,6},{5,7},{6,4},{7,5},{8,10},{9,11},{10,... | collective-permute-start | bytes 98312 | tf_op jit(solution)/shard_map/ppermute | solution.py:298
  5.8 6.7 %collective-permute-start = (bf16[8,32,64]{2,1,0:T(8,128)(2,1)}, bf16[8,32,64]{2,1,0:T(8,128)(2,1)S(1)}, u32[]{:S(2)}, u32[]{:S(2)}) collective-permute-start(bf16[8,32,64]{2,1,0:T(8,128)(2,1)} %x_ref.3), channel_id=1, source_target_pairs={{0,1},{1,2},{2,3},{3,0},{4,5},{5,6},{6,7},{7,4},{8,9},{9,10},{10,1... | collective-permute-start | bytes 98312 | tf_op jit(solution)/shard_map/ppermute | solution.py:298
  14.0 3.9 %copy-start.10 = (bf16[16,32,128]{2,1,0:T(8,128)(2,1)S(1)}, bf16[16,32,128]{2,1,0:T(8,128)(2,1)}, u32[]{:S(2)}) copy-start(bf16[16,32,128]{2,1,0:T(8,128)(2,1)} %pair_ref.1) | copy-start | bytes 393220
  14.0 8.7 %copy-start.2 = (bf16[64,256]{1,0:T(8,128)(2,1)S(1)}, bf16[64,256]{1,0:T(8,128)(2,1)}, u32[]{:S(2)}) copy-start(bf16[64,256]{1,0:T(8,128)(2,1)} %wv_ref.1) | copy-start | bytes 98308
  14.0 8.7 %copy-start.3 = (bf16[64,256]{1,0:T(8,128)(2,1)S(1)}, bf16[64,256]{1,0:T(8,128)(2,1)}, u32[]{:S(2)}) copy-start(bf16[64,256]{1,0:T(8,128)(2,1)} %wg_ref.1) | copy-start | bytes 98308
  14.0 14.1 %all-to-all-start = ((bf16[8,8,3072]{2,1,0:T(8,128)(2,1)}), bf16[8,8,3072]{2,1,0:T(8,128)(2,1)S(1)}, u32[]{:S(2)}, u32[]{:S(2)}) async-start(bf16[8,8,3072]{2,1,0:T(8,128)(2,1)} %get-tuple-element.20), calls=%async_computation | async-start | bytes 786432 | tf_op jit(solution)/shard_map/all_to_all | solution.py:317
  17.9 9.8 %collective-permute-start.3 = (bf16[16,32,128]{2,1,0:T(8,128)(2,1)S(1)}, bf16[16,32,128]{2,1,0:T(8,128)(2,1)S(1)}, u32[]{:S(2)}, u32[]{:S(2)}) collective-permute-start(bf16[16,32,128]{2,1,0:T(8,128)(2,1)S(1)} %copy-done.10), channel_id=1, source_target_pairs={{0,24},{1,16},{2,8},{3,0},{4,28},{5,20},{6,12},{7,4},{8,17},{9,25}... | collective-permute-start | bytes 393224 | tf_op jit(solution)/shard_map/ppermute | solution.py:299
  23.1 5.1 %copy-start = (bf16[1024,128]{1,0:T(8,128)(2,1)S(1)}, bf16[1024,128]{1,0:T(8,128)(2,1)}, u32[]{:S(2)}) copy-start(bf16[1024,128]{1,0:T(8,128)(2,1)} %mean_ref.3) | copy-start | bytes 786436
  28.2 0.7 %copy-start.6 = (f32[128,8]{0,1:T(8,128)S(1)}, f32[128,8]{0,1:T(8,128)}, u32[]{:S(2)}) copy-start(f32[128,8]{0,1:T(8,128)} %param.18) | copy-start | bytes 12292
  28.8 9.9 %copy-start.9 = (bf16[128,1024]{1,0:T(8,128)(2,1)S(1)}, bf16[128,1024]{1,0:T(8,128)(2,1)}, u32[]{:S(2)}) copy-start(bf16[128,1024]{1,0:T(8,128)(2,1)} %win_ref.1) | copy-start | bytes 786436
  31.2 7.6 %copy-start.11 = (bf16[512,128]{1,0:T(8,128)(2,1)S(1)}, bf16[512,128]{1,0:T(8,128)(2,1)}, u32[]{:S(2)}) copy-start(bf16[512,128]{1,0:T(8,128)(2,1)} %wout_ref.1) | copy-start | bytes 393220
  31.2 12.7 %all-to-all-start.1 = ((bf16[8,40,128]{2,1,0:T(8,128)(2,1)}), bf16[8,40,128]{2,1,0:T(8,128)(2,1)S(1)}, u32[]{:S(2)}, u32[]{:S(2)}) async-start(bf16[8,40,128]{2,1,0:T(8,128)(2,1)} %shard_map.135), calls=%async_computation.1 | async-start | bytes 163840 | tf_op jit(solution)/shard_map/all_to_all | solution.py:335
  38.8 5.1 %copy-start.4 = (bf16[256,64]{0,1:T(8,128)(2,1)S(1)}, bf16[256,64]{0,1:T(8,128)(2,1)}, u32[]{:S(2)}) copy-start(bf16[256,64]{0,1:T(8,128)(2,1)} %param.21) | copy-start | bytes 98308
